TPU v7x, 128 devices: a whole 4x4x4 slice. The times are simulated.
128 devices in a mesh: node: 64 (over z, y, x), hand: 2 (over core).
Axes of the slice: x: 4, y: 4, z: 4, core: 2. Of those that a mesh axis runs over, the one named last changes fastest.
Arguments:
- ranges: bfloat16 [2048, 128, 1326], P('node', None, 'hand'), may hold values from 0.00019931793 to 0.0039978027
- strengths: int32 [2048, 1326], P('node'), may hold values from 0 to 399
- live_hands: int32 [2048, 1326], P('node'), may hold values 0 or 1
- pot_sizes: float32 [2048, 128], P('node'), may hold values from 1 to 16
- action_counts: int32 [2048], P('node'), may hold values from 1 to 8
- parents: int32 [2048], P('node'), may hold values from 0 to 255
- turn_counts: int32 [64], replicated, may hold values from 1 to 4
- root_reach: float32 [64, 2, 1326], P(None, None, 'hand'), may hold values from 0.01 to 1
Outputs:
- turn_values: float32 [64, 2, 1326], P('node', None, 'hand')
- exploitability: float32 [], replicated
All inputs are finite; a program needn't handle non-finite values. No bound on the sum of `live_hands` on one device may be relied on, other than what follows from the above.
Results may differ from a plain program's by a relative error of at most 0.0003.
Values may be sent and summed in bfloat16 or wider, within the bound.
A program may use at most 128 MiB of HBM per device.

v0:
```python
import functools
import jax
import jax.numpy as jnp
import numpy as np
from jax import lax
from jax.sharding import Mesh
from jax.sharding import PartitionSpec as P

ACT = 8
GROUPS = 8
TACT = 4
NODE = ("node_0", "node_1", "node_2")
NODE_HAND = ("node_0", "node_1", "node_2", "hand")


def cut_along(shard, dim, count):
    before, after = (shard.shape[:dim], shard.shape[dim + 1 :])
    return jnp.moveaxis(shard.reshape(*before, count, -1, *after), dim, 0)


def sent_and_summed(shard, axis, dim):
    count = lax.axis_size(axis)
    parts = lax.all_to_all(cut_along(shard, dim, count), axis, 0, 0, tiled=True)
    return jnp.sum(parts, axis=0)


def one_axis_at_a_time(shard, axes):
    return functools.reduce(lax.psum, axes, shard)


def card_pairs(wanted):
    first_list = []
    second_list = []
    for lower_card in range(52):
        for upper_card in range(lower_card + 1, 52):
            first_list.append(lower_card)
            second_list.append(upper_card)
    return (
        jnp.asarray(np.array(first_list[:wanted], dtype=np.int32)),
        jnp.asarray(np.array(second_list[:wanted], dtype=np.int32)),
    )


def pair_compat(row_first, row_second, col_first, col_second):
    shared = (row_first[:, None] == col_first[None, :]) | (
        row_first[:, None] == col_second[None, :]
    )
    shared = (
        shared
        | (row_second[:, None] == col_first[None, :])
        | (row_second[:, None] == col_second[None, :])
    )
    return jnp.where(shared, 0.0, 1.0).astype(jnp.float32)


def showdown_block(compat, packed):
    left_strength, left_live, right_strength, right_live, reach_block = packed
    signs = jnp.sign((left_strength[:, :, None] - right_strength[:, None, :]).astype(jnp.float32))
    matrix = (signs * compat[None] * left_live[:, :, None] * right_live[:, None, :]).astype(
        jnp.bfloat16
    )
    return jnp.einsum("nij,nlj->nli", matrix, reach_block, preferred_element_type=jnp.float32)


def river_from(raw_values, pots, legal):
    count = raw_values.shape[0]
    width = raw_values.shape[2]
    values = (raw_values * pots[:, :, None]).reshape(count, 2, GROUPS, ACT, width)
    usable = jnp.arange(ACT)[None, :] < legal[:, None]
    return jnp.where(usable[:, None, None, :, None], values, -1e30).max(axis=3).sum(axis=2)


def turn_best(sums, legal):
    hand_half = sums.shape[1] // 2
    shaped = sums.reshape(-1, TACT, 2, hand_half)
    usable = jnp.arange(TACT)[None, :] < legal[:, None]
    return jnp.where(usable[:, :, None, None], shaped, -1e30).max(axis=1)


def local(
    ranges, strengths, live_hands, pot_sizes, action_counts, parents, turn_counts, root_reach
):
    node_count, line_cols, hand_half = ranges.shape
    hands_all = strengths.shape[1]
    hand_start = lax.axis_index("hand") * hand_half
    first_card, second_card = card_pairs(hands_all)
    live_all = live_hands.astype(jnp.float32)
    blocks = node_count // 4

    def grouped(array):
        return array.reshape((blocks, 4) + array.shape[1:])

    row_first = lax.dynamic_slice_in_dim(first_card, hand_start, hand_half, 0)
    row_second = lax.dynamic_slice_in_dim(second_card, hand_start, hand_half, 0)
    row_strength = lax.dynamic_slice_in_dim(strengths, hand_start, hand_half, 1)
    row_live = lax.dynamic_slice_in_dim(live_all, hand_start, hand_half, 1)
    compat = pair_compat(row_first, row_second, first_card, second_card)

    def one_block(packed):
        return showdown_block(compat, packed)

    added = lax.map(
        one_block,
        (
            grouped(row_strength),
            grouped(row_live),
            grouped(strengths),
            grouped(live_all),
            grouped(lax.all_gather(ranges, "hand", axis=2, tiled=True)),
        ),
    )
    raw_values = added.reshape(jnp.zeros((node_count, line_cols, hand_half), jnp.float32).shape)
    river_best = river_from(raw_values, pot_sizes, action_counts)
    flat_best = river_best.reshape(node_count, 2 * hand_half)
    turns_all = turn_counts.shape[0]
    turns_mine = turns_all // lax.axis_size(NODE)
    turn_start = lax.axis_index(NODE) * turns_mine
    rows_mine = turns_mine * TACT
    targets = jnp.arange(rows_mine * lax.axis_size(NODE), dtype=jnp.int32)
    onehot = (parents[None, :] == targets[:, None]).astype(jnp.float32)
    mine = sent_and_summed(jnp.dot(onehot, flat_best, precision=lax.Precision.HIGHEST), NODE, 0)
    legal_mine = lax.dynamic_slice_in_dim(turn_counts, turn_start, turns_mine, 0)
    turn_values = turn_best(mine, legal_mine)
    reach_mine = lax.dynamic_slice_in_dim(root_reach, turn_start, turns_mine, 0)
    exploitability = one_axis_at_a_time(jnp.sum(reach_mine * turn_values), NODE_HAND)
    return (turn_values, exploitability)


def solution(mesh):
    split = Mesh(
        mesh.devices.reshape(4, 4, 4, mesh.shape["hand"]), ("node_0", "node_1", "node_2", "hand")
    )
    in_specs = (
        P(NODE, None, "hand"),
        P(NODE, None),
        P(NODE, None),
        P(NODE, None),
        P(NODE),
        P(NODE),
        P(),
        P(None, None, "hand"),
    )
    out_specs = (P(NODE, None, "hand"), P())
    return jax.shard_map(local, mesh=split, in_specs=in_specs, out_specs=out_specs, check_vma=False)
```

profile of v0, /device:TPU:1, one launch (start us, length us, event | category | flops | bytes accessed | tf_op | source)
XLA Modules:
  0.0 228.3 jit_solution(14435566055462864649)
XLA Ops:
  7.2 0.7 all-gather.2.cloned.1.call-update
  8.0 0.9 convert_element_type.10
  9.1 1.0 reshape.101
  10.1 1.0 constant_dynamic-slice_fusion.2
  11.1 0.8 dynamic_slice.40
  11.9 0.8 dynamic_slice.41
  12.7 0.8 copy.24
  13.7 25.3 %all-gather.2.cloned.1.call-done = bf16[32,128,1326]{1,0,2:T(8,128)(2,1)} async-done(((bf16[32,128,663]{1,0,2:T(8,128)(2,1)}), bf16[32,128,1326]{1,0,2:T(8,128)(2,1)}) %all-gather.2.cloned.1.call-update) | async-done | bytes 10862608 | tf_op jit(solution)/shard_map/all_gather | solution.py:109
  39.1 84.1 %while.11 = (s32[]{:T(128)}, f32[8,4,128,663]{2,3,1,0:T(8,128)}, bf16[8,4,128,1326]{2,1,0,3:T(4,128)(2,1)}, s32[8,4,663]{2,1,0:T(4,128)S(1)}, s32[8,4,1326]{2,1,...) while((s32[]{:T(128)}, f32[8,4,128,663]{2,3,1,0:T(8,128)}, ...), condition=%wide.region_1.2_spmd.clone, body=%wide.region_0.1_spmd.clone.sunk | while | flops 931886272 | bytes 12673953 | solution.py:102
  39.1 1.6 constant_dynamic-slice_fusion.4
  40.7 1.5 or_select_fusion.2
  42.3 7.3 %fusion.11 = f32[8,4,128,663]{2,3,1,0:T(8,128)} fusion(f32[8,4,128,663]{2,3,1,0:T(8,128)} %get-tuple-element.197, s32[]{:T(128)} %get-tuple-element.196, f32[4,1326]{1,0:T(4,128)S(1)} %dynamic-slice_bitcast_fusion.8, f32[4,663]{1,0:T(4,128)S(1)} %dynamic-slice_bitcast_fusion.9, f32[663,1326]{1,0:T(8,128)S(1)} %or_select_fusion.2, ...), kind=kOutput, calls=%fused_computation.5.clone.1 | convolution fusion | flops 924853184 | bytes 6298408 | tf_op jit(solution)/shard_map/while/body/eval_jaxpr/nij,nlj->nli/dot_general | solution.py:62
  49.6 1.6 constant_dynamic-slice_fusion.4
  51.3 1.5 or_select_fusion.2
  52.8 7.3 %fusion.11 = f32[8,4,128,663]{2,3,1,0:T(8,128)} fusion(f32[8,4,128,663]{2,3,1,0:T(8,128)} %get-tuple-element.197, s32[]{:T(128)} %get-tuple-element.196, f32[4,1326]{1,0:T(4,128)S(1)} %dynamic-slice_bitcast_fusion.8, f32[4,663]{1,0:T(4,128)S(1)} %dynamic-slice_bitcast_fusion.9, f32[663,1326]{1,0:T(8,128)S(1)} %or_select_fusion.2, ...), kind=kOutput, calls=%fused_computation.5.clone.1 | convolution fusion | flops 924853184 | bytes 6298408 | tf_op jit(solution)/shard_map/while/body/eval_jaxpr/nij,nlj->nli/dot_general | solution.py:62
  60.1 1.6 constant_dynamic-slice_fusion.4
  61.8 1.5 or_select_fusion.2
  63.3 7.3 %fusion.11 = f32[8,4,128,663]{2,3,1,0:T(8,128)} fusion(f32[8,4,128,663]{2,3,1,0:T(8,128)} %get-tuple-element.197, s32[]{:T(128)} %get-tuple-element.196, f32[4,1326]{1,0:T(4,128)S(1)} %dynamic-slice_bitcast_fusion.8, f32[4,663]{1,0:T(4,128)S(1)} %dynamic-slice_bitcast_fusion.9, f32[663,1326]{1,0:T(8,128)S(1)} %or_select_fusion.2, ...), kind=kOutput, calls=%fused_computation.5.clone.1 | convolution fusion | flops 924853184 | bytes 6298408 | tf_op jit(solution)/shard_map/while/body/eval_jaxpr/nij,nlj->nli/dot_general | solution.py:62
  70.6 1.6 constant_dynamic-slice_fusion.4
  72.3 1.5 or_select_fusion.2
  73.9 7.3 %fusion.11 = f32[8,4,128,663]{2,3,1,0:T(8,128)} fusion(f32[8,4,128,663]{2,3,1,0:T(8,128)} %get-tuple-element.197, s32[]{:T(128)} %get-tuple-element.196, f32[4,1326]{1,0:T(4,128)S(1)} %dynamic-slice_bitcast_fusion.8, f32[4,663]{1,0:T(4,128)S(1)} %dynamic-slice_bitcast_fusion.9, f32[663,1326]{1,0:T(8,128)S(1)} %or_select_fusion.2, ...), kind=kOutput, calls=%fused_computation.5.clone.1 | convolution fusion | flops 924853184 | bytes 6298408 | tf_op jit(solution)/shard_map/while/body/eval_jaxpr/nij,nlj->nli/dot_general | solution.py:62
  81.1 1.6 constant_dynamic-slice_fusion.4
  82.8 1.5 or_select_fusion.2
  84.3 7.3 %fusion.11 = f32[8,4,128,663]{2,3,1,0:T(8,128)} fusion(f32[8,4,128,663]{2,3,1,0:T(8,128)} %get-tuple-element.197, s32[]{:T(128)} %get-tuple-element.196, f32[4,1326]{1,0:T(4,128)S(1)} %dynamic-slice_bitcast_fusion.8, f32[4,663]{1,0:T(4,128)S(1)} %dynamic-slice_bitcast_fusion.9, f32[663,1326]{1,0:T(8,128)S(1)} %or_select_fusion.2, ...), kind=kOutput, calls=%fused_computation.5.clone.1 | convolution fusion | flops 924853184 | bytes 6298408 | tf_op jit(solution)/shard_map/while/body/eval_jaxpr/nij,nlj->nli/dot_general | solution.py:62
  91.7 1.6 constant_dynamic-slice_fusion.4
  93.3 1.5 or_select_fusion.2
  94.9 7.3 %fusion.11 = f32[8,4,128,663]{2,3,1,0:T(8,128)} fusion(f32[8,4,128,663]{2,3,1,0:T(8,128)} %get-tuple-element.197, s32[]{:T(128)} %get-tuple-element.196, f32[4,1326]{1,0:T(4,128)S(1)} %dynamic-slice_bitcast_fusion.8, f32[4,663]{1,0:T(4,128)S(1)} %dynamic-slice_bitcast_fusion.9, f32[663,1326]{1,0:T(8,128)S(1)} %or_select_fusion.2, ...), kind=kOutput, calls=%fused_computation.5.clone.1 | convolution fusion | flops 924853184 | bytes 6298408 | tf_op jit(solution)/shard_map/while/body/eval_jaxpr/nij,nlj->nli/dot_general | solution.py:62
  102.2 1.6 constant_dynamic-slice_fusion.4
  103.9 1.5 or_select_fusion.2
  105.4 7.3 %fusion.11 = f32[8,4,128,663]{2,3,1,0:T(8,128)} fusion(f32[8,4,128,663]{2,3,1,0:T(8,128)} %get-tuple-element.197, s32[]{:T(128)} %get-tuple-element.196, f32[4,1326]{1,0:T(4,128)S(1)} %dynamic-slice_bitcast_fusion.8, f32[4,663]{1,0:T(4,128)S(1)} %dynamic-slice_bitcast_fusion.9, f32[663,1326]{1,0:T(8,128)S(1)} %or_select_fusion.2, ...), kind=kOutput, calls=%fused_computation.5.clone.1 | convolution fusion | flops 924853184 | bytes 6298408 | tf_op jit(solution)/shard_map/while/body/eval_jaxpr/nij,nlj->nli/dot_general | solution.py:62
  112.7 1.6 constant_dynamic-slice_fusion.4
  114.3 1.5 or_select_fusion.2
  115.9 7.3 %fusion.11 = f32[8,4,128,663]{2,3,1,0:T(8,128)} fusion(f32[8,4,128,663]{2,3,1,0:T(8,128)} %get-tuple-element.197, s32[]{:T(128)} %get-tuple-element.196, f32[4,1326]{1,0:T(4,128)S(1)} %dynamic-slice_bitcast_fusion.8, f32[4,663]{1,0:T(4,128)S(1)} %dynamic-slice_bitcast_fusion.9, f32[663,1326]{1,0:T(8,128)S(1)} %or_select_fusion.2, ...), kind=kOutput, calls=%fused_computation.5.clone.1 | convolution fusion | flops 924853184 | bytes 6298408 | tf_op jit(solution)/shard_map/while/body/eval_jaxpr/nij,nlj->nli/dot_general | solution.py:62
  123.2 12.0 %copy.23 = f32[8,4,128,663]{3,2,1,0:T(8,128)} copy(f32[8,4,128,663]{2,3,1,0:T(8,128)} %get-tuple-element.44) | data formatting | bytes 21725184 | tf_op jit(solution)/shard_map/while | solution.py:102
  135.1 16.8 %select_reduce_fusion = f32[32,2,8,663]{3,2,1,0:T(8,128)S(1)} fusion(f32[32,2,8,8,663]{4,3,2,1,0:T(8,128)} %bitcast.32, f32[32,2,8,8]{3,2,1,0:T(8,128)S(1)} %copy.25, pred[32,8]{1,0:T(8,128)(4,1)S(1)} %iota_compare_fusion), kind=kLoop, calls=%fused_computation.12 | loop fusion | flops 7807488 | bytes 12237056 | tf_op jit(solution)/shard_map/reduce_max | solution.py:70
  152.0 0.5 reduce_sum.27
  152.6 0.8 fusion.5
  153.5 2.0 copy.26
  155.5 10.1 %all-to-all-start = ((f32[64,4,1326]{2,1,0:T(4,128)}), f32[64,4,1326]{2,1,0:T(4,128)S(1)}, u32[]{:S(2)}, u32[]{:S(2)}) async-start(f32[64,4,1326]{2,1,0:T(4,128)} %copy.26), calls=%async_computation | async-start | bytes 2883584 | tf_op jit(solution)/shard_map/all_to_all | solution.py:23
  165.7 0.6 dynamic_slice.38
  166.3 0.6 iota_compare_fusion.1
  166.9 21.1 %all-to-all-done = f32[64,4,1326]{2,1,0:T(4,128)S(1)} async-done(((f32[64,4,1326]{2,1,0:T(4,128)}), f32[64,4,1326]{2,1,0:T(4,128)S(1)}, u32[]{:S(2)}, u32[]{:S(2)}) %all-to-all-start) | async-done | bytes 1357856 | tf_op jit(solution)/shard_map/all_to_all | solution.py:23
  188.0 0.3 reduce_sum.28
  188.5 1.3 multiply_reduce_fusion
  189.8 7.1 %psum.28 = f32[]{:T(128)} all-reduce(f32[]{:T(128)} %multiply_reduce_fusion), channel_id=1, replica_groups=mesh['node_0'=4,'node_1'=4,'node_2'=4,'hand'=2] {'node_0'}, use_global_device_ids=true, to_apply=%region_7.8 | all-reduce | flops 1 | bytes 8 | tf_op jit(solution)/shard_map/psum | solution.py:28
  196.9 7.5 %psum.29 = f32[]{:T(128)} all-reduce(f32[]{:T(128)} %psum.28), channel_id=1, replica_groups=mesh['node_0'=4,'node_1'=4,'node_2'=4,'hand'=2] {'node_1'}, use_global_device_ids=true, to_apply=%region_8.9 | all-reduce | flops 1 | bytes 8 | tf_op jit(solution)/shard_map/psum | solution.py:28
  204.4 6.9 %psum.30 = f32[]{:T(128)} all-reduce(f32[]{:T(128)} %psum.29), channel_id=1, replica_groups=mesh['node_0'=4,'node_1'=4,'node_2'=4,'hand'=2] {'node_2'}, use_global_device_ids=true, to_apply=%region_9.10 | all-reduce | flops 1 | bytes 8 | tf_op jit(solution)/shard_map/psum | solution.py:28
  211.3 10.2 %psum.31 = f32[]{:T(128)} all-reduce(f32[]{:T(128)} %psum.30), channel_id=1, replica_groups=mesh['node_0'=4,'node_1'=4,'node_2'=4,'hand'=2] {'hand'}, use_global_device_ids=true, to_apply=%region_10.11 | all-reduce | flops 1 | bytes 8 | tf_op jit(solution)/shard_map/psum | solution.py:28
  (56 shorter events, 1.2 us)
Async XLA Ops:
  7.2 31.9 %copy-start = (s32[1326]{0:T(1024)S(1)}, s32[1326]{0:T(1024)}, u32[]{:S(2)}) copy-start(s32[1326]{0:T(1024)} %constant.58.clone) | copy-start | bytes 15916
  7.2 31.9 %copy-start.1 = (s32[1326]{0:T(1024)S(1)}, s32[1326]{0:T(1024)}, u32[]{:S(2)}) copy-start(s32[1326]{0:T(1024)} %constant.59.clone) | copy-start | bytes 15916
  7.2 6.5 %copy-start.4 = (s32[32]{0:T(128)S(1)}, s32[32]{0:T(128)}, u32[]{:S(2)}) copy-start(s32[32]{0:T(128)} %param.16) | copy-start | bytes 388
  7.2 31.9 %all-gather.2.cloned.1.call-start = ((), (), s32[]{:S(2)}) async-start(), calls=%async_computation.1 | async-start | bytes 16293888 | tf_op jit(solution)/shard_map/all_gather | solution.py:109
  135.1 17.5 %copy-start.3 = (s32[32]{0:T(128)S(1)}, s32[32]{0:T(128)}, u32[]{:S(2)}) copy-start(s32[32]{0:T(128)} %param.17) | copy-start | bytes 388
  152.0 13.7 %copy-start.5 = (s32[64]{0:T(128)S(1)}, s32[64]{0:T(128)}, u32[]{:S(2)}) copy-start(s32[64]{0:T(128)} %param.18) | copy-start | bytes 772
  155.5 32.5 %all-to-all-start = ((f32[64,4,1326]{2,1,0:T(4,128)}), f32[64,4,1326]{2,1,0:T(4,128)S(1)}, u32[]{:S(2)}, u32[]{:S(2)}) async-start(f32[64,4,1326]{2,1,0:T(4,128)} %copy.26), calls=%async_computation | async-start | bytes 2883584 | tf_op jit(solution)/shard_map/all_to_all | solution.py:23
  188.5 33.0 %copy-start.2 = (f32[1,2,663]{2,1,0:T(2,128)}, f32[1,2,663]{2,1,0:T(2,128)S(1)}, u32[]{:S(2)}) copy-start(f32[1,2,663]{2,1,0:T(2,128)S(1)} %reduce_max.22) | copy-start | bytes 15916
Sparse Core Ops, SparseCore 0:
  9.7 29.3 all-gather.1
where the time goes:
time: 229 us; the launch traced here: 228 us
  matrix products  59.2 us (26%)
  waiting for transfers between devices  47.1 us (21%)
  other arithmetic  32.8 us (14%)
  local copies, waits for them, and re-layouts  32.7 us (14%)
  blocking collectives  31.7 us (14%)
  between operations  14.2 us (6%)
  starting transfers between devices  10.2 us (4%)
    dot_general x8, matrix products, showdown_block(): jnp.einsum('nij,nlj->nli', matrix, reach_block, preferred_element_type=jn...  58.4 us
    psum x4, blocking collectives, one_axis_at_a_time(): return functools.reduce(lax.psum, axes, shard)  31.7 us
    all_gather x1, waiting for transfers between devices, local(): lax.all_gather(ranges, 'hand', axis=2, tiled=True)  25.3 us
    all_to_all x1, waiting for transfers between devices, sent_and_summed(): parts = lax.all_to_all(cut_along(shard, dim, count), axis, 0, 0, tiled=True)  21.1 us
    reduce_max x1, other arithmetic, river_from(): jnp.where(usable[:, None, None, :, None], values, -1e+30).max(axis=3)  16.8 us
    dynamic_slice x8, local copies, waits for them, and re-layouts, local(): lax.map(one_block, (grouped(row_strength), grouped(row_live), grouped(str...  12.8 us
    select_n x8, other arithmetic, pair_compat(): return jnp.where(shared, 0.0, 1.0).astype(jnp.float32)  12.2 us
    while x1, local copies, waits for them, and re-layouts, local(): lax.map(one_block, (grouped(row_strength), grouped(row_live), grouped(str...  12 us
  transfers between devices with their start and end apart: 2, of which 2 were waited for; matrix products, arithmetic and copies ran while one was open for 3% of the time, Pallas kernels for 0%

commit v1 on v0

--- a/solution.py
+++ b/solution.py
@@ -106,7 +106,12 @@
             grouped(row_live),
             grouped(strengths),
             grouped(live_all),
-            grouped(lax.all_gather(ranges, "hand", axis=2, tiled=True)),
+            grouped(
+                jnp.concatenate(
+                    lax.all_to_all(jnp.stack([ranges] * lax.axis_size("hand")), "hand", 0, 0),
+                    axis=2,
+                )
+            ),
         ),
     )
     raw_values = added.reshape(jnp.zeros((node_count, line_cols, hand_half), jnp.float32).shape)

time: 229 us -> 214 us (0.934)
  waiting for transfers between devices: 47.1 us -> 29.3 us
  between operations: 14.2 us -> 0.8 us
  starting transfers between devices: 10.2 us -> 20.5 us
  other arithmetic: 32.8 us -> 42.5 us
  local copies, waits for them, and re-layouts: 32.7 us -> 28.9 us
    all_gather x1 -> x0, waiting for transfers between devices: 25.3 us -> none  [local(): lax.all_gather(ranges, 'hand', axis=2, tiled=True)]
    another operation x0 -> x1, other arithmetic: none -> 10.6 us  [local(): jnp.stack([ranges] * lax.axis_size('hand'))]
    all_to_all x0 -> x1, starting transfers between devices: none -> 9.3 us  [local(): lax.all_to_all(jnp.stack([ranges] * lax.axis_size('hand')), 'hand', 0, 0)]
    all_to_all x0 -> x1, waiting for transfers between devices: none -> 8.28 us  [local(): lax.all_to_all(jnp.stack([ranges] * lax.axis_size('hand')), 'hand', 0, 0)]
  transfers between devices with their start and end apart: 2 -> 2, of which waited for: 2 -> 2; matrix products, arithmetic and copies ran while one was open for 3% -> 1% of each run, Pallas kernels for 0% -> 0%
where the time goes in v1:
time: 214 us; the launch traced here: 213 us
  matrix products  59.2 us (28%)
  other arithmetic  42.5 us (20%)
  blocking collectives  31.8 us (15%)
  waiting for transfers between devices  29.3 us (14%)
  local copies, waits for them, and re-layouts  28.9 us (14%)
  starting transfers between devices  20.5 us (10%)
    dot_general x8, matrix products, showdown_block(): jnp.einsum('nij,nlj->nli', matrix, reach_block, preferred_element_type=jn...  58.4 us
    psum x4, blocking collectives, one_axis_at_a_time(): return functools.reduce(lax.psum, axes, shard)  31.8 us
    all_to_all x1, waiting for transfers between devices, sent_and_summed(): parts = lax.all_to_all(cut_along(shard, dim, count), axis, 0, 0, tiled=True)  21 us
    reduce_max x1, other arithmetic, river_from(): jnp.where(usable[:, None, None, :, None], values, -1e+30).max(axis=3)  16.8 us
    dynamic_slice x8, local copies, waits for them, and re-layouts, local(): lax.map(one_block, (grouped(row_strength), grouped(row_live), grouped(str...  12.8 us
    select_n x8, other arithmetic, pair_compat(): return jnp.where(shared, 0.0, 1.0).astype(jnp.float32)  12.2 us
    while x1, local copies, waits for them, and re-layouts, local(): lax.map(one_block, (grouped(row_strength), grouped(row_live), grouped(str...  12 us
    all_to_all x1, starting transfers between devices, sent_and_summed(): parts = lax.all_to_all(cut_along(shard, dim, count), axis, 0, 0, tiled=True)  11.2 us
  transfers between devices with their start and end apart: 2, of which 2 were waited for; matrix products, arithmetic and copies ran while one was open for 1% of the time, Pallas kernels for 0%

profile of v1, /device:TPU:1, one launch (start us, length us, event | category | flops | bytes accessed | tf_op | source)
XLA Modules:
  0.0 213.4 jit_solution(6697935267795248760)
XLA Ops:
  0.6 10.6 %pad_maximum_fusion = bf16[2,32,128,663]{2,1,3,0:T(8,128)(2,1)} fusion(bf16[1,32,128,663]{2,1,3,0:T(8,128)(2,1)} %bitcast.36), kind=kLoop, calls=%fused_computation.13 | loop fusion | flops 5431296 | bytes 16293888 | tf_op jit(solution)/shard_map/stack | solution.py:111
  11.3 9.3 %all-to-all-start = ((bf16[2,32,128,663]{2,1,3,0:T(8,128)(2,1)}), bf16[2,32,128,663]{2,1,3,0:T(8,128)(2,1)}, u32[]{:S(2)}, u32[]{:S(2)}) async-start(bf16[2,32,128,663]{2,1,3,0:T(8,128)(2,1)} %pad_maximum_fusion), calls=%async_computation | async-start | bytes 21725184 | tf_op jit(solution)/shard_map/all_to_all | solution.py:111
  20.6 0.1 constant_dynamic-slice_fusion.1
  20.7 0.1 constant_dynamic-slice_fusion.2
  21.2 8.3 %all-to-all-done = bf16[2,32,128,663]{2,1,3,0:T(8,128)(2,1)} async-done(((bf16[2,32,128,663]{2,1,3,0:T(8,128)(2,1)}), bf16[2,32,128,663]{2,1,3,0:T(8,128)(2,1)}, u32[]{:S(2)}, u32[]{:S(2)}) %all-to-all-start) | async-done | bytes 10862624 | tf_op jit(solution)/shard_map/all_to_all | solution.py:111
  29.4 84.1 %while.11 = (s32[]{:T(128)}, f32[8,4,128,663]{2,3,1,0:T(8,128)}, bf16[8,4,128,1326]{2,1,0,3:T(4,128)(2,1)}, s32[8,4,663]{2,1,0:T(4,128)S(1)}, s32[8,4,1326]{2,1,...) while((s32[]{:T(128)}, f32[8,4,128,663]{2,3,1,0:T(8,128)}, ...), condition=%wide.region_1.2_spmd.clone, body=%wide.region_0.1_spmd.clone.sunk | while | flops 931886272 | bytes 12673953 | solution.py:102
  29.4 1.6 constant_dynamic-slice_fusion.4
  31.1 1.5 or_select_fusion.2
  32.7 7.3 %fusion.11 = f32[8,4,128,663]{2,3,1,0:T(8,128)} fusion(f32[8,4,128,663]{2,3,1,0:T(8,128)} %get-tuple-element.208, s32[]{:T(128)} %get-tuple-element.207, f32[4,1326]{1,0:T(4,128)S(1)} %dynamic-slice_bitcast_fusion.8, f32[4,663]{1,0:T(4,128)S(1)} %dynamic-slice_bitcast_fusion.9, f32[663,1326]{1,0:T(8,128)S(1)} %or_select_fusion.2, ...), kind=kOutput, calls=%fused_computation.5.clone.1 | convolution fusion | flops 924853184 | bytes 6298408 | tf_op jit(solution)/shard_map/while/body/eval_jaxpr/nij,nlj->nli/dot_general | solution.py:62
  39.9 1.6 constant_dynamic-slice_fusion.4
  41.6 1.5 or_select_fusion.2
  43.2 7.3 %fusion.11 = f32[8,4,128,663]{2,3,1,0:T(8,128)} fusion(f32[8,4,128,663]{2,3,1,0:T(8,128)} %get-tuple-element.208, s32[]{:T(128)} %get-tuple-element.207, f32[4,1326]{1,0:T(4,128)S(1)} %dynamic-slice_bitcast_fusion.8, f32[4,663]{1,0:T(4,128)S(1)} %dynamic-slice_bitcast_fusion.9, f32[663,1326]{1,0:T(8,128)S(1)} %or_select_fusion.2, ...), kind=kOutput, calls=%fused_computation.5.clone.1 | convolution fusion | flops 924853184 | bytes 6298408 | tf_op jit(solution)/shard_map/while/body/eval_jaxpr/nij,nlj->nli/dot_general | solution.py:62
  50.5 1.6 constant_dynamic-slice_fusion.4
  52.1 1.5 or_select_fusion.2
  53.7 7.3 %fusion.11 = f32[8,4,128,663]{2,3,1,0:T(8,128)} fusion(f32[8,4,128,663]{2,3,1,0:T(8,128)} %get-tuple-element.208, s32[]{:T(128)} %get-tuple-element.207, f32[4,1326]{1,0:T(4,128)S(1)} %dynamic-slice_bitcast_fusion.8, f32[4,663]{1,0:T(4,128)S(1)} %dynamic-slice_bitcast_fusion.9, f32[663,1326]{1,0:T(8,128)S(1)} %or_select_fusion.2, ...), kind=kOutput, calls=%fused_computation.5.clone.1 | convolution fusion | flops 924853184 | bytes 6298408 | tf_op jit(solution)/shard_map/while/body/eval_jaxpr/nij,nlj->nli/dot_general | solution.py:62
  61.0 1.6 constant_dynamic-slice_fusion.4
  62.6 1.5 or_select_fusion.2
  64.2 7.3 %fusion.11 = f32[8,4,128,663]{2,3,1,0:T(8,128)} fusion(f32[8,4,128,663]{2,3,1,0:T(8,128)} %get-tuple-element.208, s32[]{:T(128)} %get-tuple-element.207, f32[4,1326]{1,0:T(4,128)S(1)} %dynamic-slice_bitcast_fusion.8, f32[4,663]{1,0:T(4,128)S(1)} %dynamic-slice_bitcast_fusion.9, f32[663,1326]{1,0:T(8,128)S(1)} %or_select_fusion.2, ...), kind=kOutput, calls=%fused_computation.5.clone.1 | convolution fusion | flops 924853184 | bytes 6298408 | tf_op jit(solution)/shard_map/while/body/eval_jaxpr/nij,nlj->nli/dot_general | solution.py:62
  71.4 1.6 constant_dynamic-slice_fusion.4
  73.1 1.5 or_select_fusion.2
  74.6 7.3 %fusion.11 = f32[8,4,128,663]{2,3,1,0:T(8,128)} fusion(f32[8,4,128,663]{2,3,1,0:T(8,128)} %get-tuple-element.208, s32[]{:T(128)} %get-tuple-element.207, f32[4,1326]{1,0:T(4,128)S(1)} %dynamic-slice_bitcast_fusion.8, f32[4,663]{1,0:T(4,128)S(1)} %dynamic-slice_bitcast_fusion.9, f32[663,1326]{1,0:T(8,128)S(1)} %or_select_fusion.2, ...), kind=kOutput, calls=%fused_computation.5.clone.1 | convolution fusion | flops 924853184 | bytes 6298408 | tf_op jit(solution)/shard_map/while/body/eval_jaxpr/nij,nlj->nli/dot_general | solution.py:62
  82.0 1.6 constant_dynamic-slice_fusion.4
  83.6 1.5 or_select_fusion.2
  85.2 7.3 %fusion.11 = f32[8,4,128,663]{2,3,1,0:T(8,128)} fusion(f32[8,4,128,663]{2,3,1,0:T(8,128)} %get-tuple-element.208, s32[]{:T(128)} %get-tuple-element.207, f32[4,1326]{1,0:T(4,128)S(1)} %dynamic-slice_bitcast_fusion.8, f32[4,663]{1,0:T(4,128)S(1)} %dynamic-slice_bitcast_fusion.9, f32[663,1326]{1,0:T(8,128)S(1)} %or_select_fusion.2, ...), kind=kOutput, calls=%fused_computation.5.clone.1 | convolution fusion | flops 924853184 | bytes 6298408 | tf_op jit(solution)/shard_map/while/body/eval_jaxpr/nij,nlj->nli/dot_general | solution.py:62
  92.5 1.6 constant_dynamic-slice_fusion.4
  94.1 1.5 or_select_fusion.2
  95.7 7.4 %fusion.11 = f32[8,4,128,663]{2,3,1,0:T(8,128)} fusion(f32[8,4,128,663]{2,3,1,0:T(8,128)} %get-tuple-element.208, s32[]{:T(128)} %get-tuple-element.207, f32[4,1326]{1,0:T(4,128)S(1)} %dynamic-slice_bitcast_fusion.8, f32[4,663]{1,0:T(4,128)S(1)} %dynamic-slice_bitcast_fusion.9, f32[663,1326]{1,0:T(8,128)S(1)} %or_select_fusion.2, ...), kind=kOutput, calls=%fused_computation.5.clone.1 | convolution fusion | flops 924853184 | bytes 6298408 | tf_op jit(solution)/shard_map/while/body/eval_jaxpr/nij,nlj->nli/dot_general | solution.py:62
  103.0 1.6 constant_dynamic-slice_fusion.4
  104.7 1.5 or_select_fusion.2
  106.2 7.3 %fusion.11 = f32[8,4,128,663]{2,3,1,0:T(8,128)} fusion(f32[8,4,128,663]{2,3,1,0:T(8,128)} %get-tuple-element.208, s32[]{:T(128)} %get-tuple-element.207, f32[4,1326]{1,0:T(4,128)S(1)} %dynamic-slice_bitcast_fusion.8, f32[4,663]{1,0:T(4,128)S(1)} %dynamic-slice_bitcast_fusion.9, f32[663,1326]{1,0:T(8,128)S(1)} %or_select_fusion.2, ...), kind=kOutput, calls=%fused_computation.5.clone.1 | convolution fusion | flops 924853184 | bytes 6298408 | tf_op jit(solution)/shard_map/while/body/eval_jaxpr/nij,nlj->nli/dot_general | solution.py:62
  113.5 12.0 %copy.23 = f32[8,4,128,663]{3,2,1,0:T(8,128)} copy(f32[8,4,128,663]{2,3,1,0:T(8,128)} %get-tuple-element.44) | data formatting | bytes 21725184 | tf_op jit(solution)/shard_map/while | solution.py:102
  125.6 0.1 copy.24
  125.7 0.2 copy.25
  125.9 16.8 %select_reduce_fusion = f32[32,2,8,663]{3,2,1,0:T(8,128)S(1)} fusion(f32[32,2,8,8,663]{4,3,2,1,0:T(8,128)} %bitcast.35, f32[32,2,8,8]{3,2,1,0:T(8,128)S(1)} %copy.25, pred[32,8]{1,0:T(8,128)(4,1)S(1)} %iota_compare_fusion), kind=kLoop, calls=%fused_computation.12 | loop fusion | flops 7807488 | bytes 12237056 | tf_op jit(solution)/shard_map/reduce_max | solution.py:70
  142.7 0.5 reduce_sum.27
  143.2 0.2 reshape.106
  143.4 0.8 fusion.5
  144.3 2.0 copy.26
  146.3 11.2 %all-to-all-start.1 = ((f32[64,4,1326]{2,1,0:T(4,128)}), f32[64,4,1326]{2,1,0:T(4,128)S(1)}, u32[]{:S(2)}, u32[]{:S(2)}) async-start(f32[64,4,1326]{2,1,0:T(4,128)} %copy.26), calls=%async_computation.1 | async-start | bytes 2883584 | tf_op jit(solution)/shard_map/all_to_all | solution.py:23
  157.6 0.6 dynamic_slice.38
  158.2 0.6 iota_compare_fusion.1
  158.8 21.0 %all-to-all-done.1 = f32[64,4,1326]{2,1,0:T(4,128)S(1)} async-done(((f32[64,4,1326]{2,1,0:T(4,128)}), f32[64,4,1326]{2,1,0:T(4,128)S(1)}, u32[]{:S(2)}, u32[]{:S(2)}) %all-to-all-start.1) | async-done | bytes 1357856 | tf_op jit(solution)/shard_map/all_to_all | solution.py:23
  179.8 0.3 reduce_sum.28
  180.3 1.3 multiply_reduce_fusion
  181.6 7.1 %psum.28 = f32[]{:T(128)} all-reduce(f32[]{:T(128)} %multiply_reduce_fusion), channel_id=1, replica_groups=mesh['node_0'=4,'node_1'=4,'node_2'=4,'hand'=2] {'node_0'}, use_global_device_ids=true, to_apply=%region_7.8 | all-reduce | flops 1 | bytes 8 | tf_op jit(solution)/shard_map/psum | solution.py:28
  188.7 7.0 %psum.29 = f32[]{:T(128)} all-reduce(f32[]{:T(128)} %psum.28), channel_id=1, replica_groups=mesh['node_0'=4,'node_1'=4,'node_2'=4,'hand'=2] {'node_1'}, use_global_device_ids=true, to_apply=%region_8.9 | all-reduce | flops 1 | bytes 8 | tf_op jit(solution)/shard_map/psum | solution.py:28
  195.7 7.4 %psum.30 = f32[]{:T(128)} all-reduce(f32[]{:T(128)} %psum.29), channel_id=1, replica_groups=mesh['node_0'=4,'node_1'=4,'node_2'=4,'hand'=2] {'node_2'}, use_global_device_ids=true, to_apply=%region_9.10 | all-reduce | flops 1 | bytes 8 | tf_op jit(solution)/shard_map/psum | solution.py:28
  203.0 10.3 %psum.31 = f32[]{:T(128)} all-reduce(f32[]{:T(128)} %psum.30), channel_id=1, replica_groups=mesh['node_0'=4,'node_1'=4,'node_2'=4,'hand'=2] {'hand'}, use_global_device_ids=true, to_apply=%region_10.11 | all-reduce | flops 1 | bytes 8 | tf_op jit(solution)/shard_map/psum | solution.py:28
  (62 shorter events, 1.0 us)
Async XLA Ops:
  11.2 9.3 %copy-start.3 = (s32[32,1326]{1,0:T(8,128)S(1)}, s32[32,1326]{1,0:T(8,128)}, u32[]{:S(2)}) copy-start(s32[32,1326]{1,0:T(8,128)} %param.14) | copy-start | bytes 509188
  11.2 9.5 %copy-start = (s32[32,1326]{1,0:T(8,128)S(1)}, s32[32,1326]{1,0:T(8,128)}, u32[]{:S(2)}) copy-start(s32[32,1326]{1,0:T(8,128)} %param.13) | copy-start | bytes 509188
  11.2 9.8 %copy-start.1 = (s32[1326]{0:T(1024)S(1)}, s32[1326]{0:T(1024)}, u32[]{:S(2)}) copy-start(s32[1326]{0:T(1024)} %constant.58.clone) | copy-start | bytes 15916
  11.2 9.8 %copy-start.2 = (s32[1326]{0:T(1024)S(1)}, s32[1326]{0:T(1024)}, u32[]{:S(2)}) copy-start(s32[1326]{0:T(1024)} %constant.59.clone) | copy-start | bytes 15916
  11.3 18.2 %all-to-all-start = ((bf16[2,32,128,663]{2,1,3,0:T(8,128)(2,1)}), bf16[2,32,128,663]{2,1,3,0:T(8,128)(2,1)}, u32[]{:S(2)}, u32[]{:S(2)}) async-start(bf16[2,32,128,663]{2,1,3,0:T(8,128)(2,1)} %pad_maximum_fusion), calls=%async_computation | async-start | bytes 21725184 | tf_op jit(solution)/shard_map/all_to_all | solution.py:111
  113.5 12.0 %copy-start.5 = (f32[32,128]{1,0:T(8,128)S(1)}, f32[32,128]{1,0:T(8,128)}, u32[]{:S(2)}) copy-start(f32[32,128]{1,0:T(8,128)} %param.15) | copy-start | bytes 49156
  113.5 12.3 %copy-start.7 = (s32[32]{0:T(128)S(1)}, s32[32]{0:T(128)}, u32[]{:S(2)}) copy-start(s32[32]{0:T(128)} %param.16) | copy-start | bytes 388
  125.6 17.8 %copy-start.6 = (s32[32]{0:T(128)S(1)}, s32[32]{0:T(128)}, u32[]{:S(2)}) copy-start(s32[32]{0:T(128)} %param.17) | copy-start | bytes 388
  125.9 31.6 %copy-start.8 = (s32[64]{0:T(128)S(1)}, s32[64]{0:T(128)}, u32[]{:S(2)}) copy-start(s32[64]{0:T(128)} %param.18) | copy-start | bytes 772
  146.3 33.5 %all-to-all-start.1 = ((f32[64,4,1326]{2,1,0:T(4,128)}), f32[64,4,1326]{2,1,0:T(4,128)S(1)}, u32[]{:S(2)}, u32[]{:S(2)}) async-start(f32[64,4,1326]{2,1,0:T(4,128)} %copy.26), calls=%async_computation.1 | async-start | bytes 2883584 | tf_op jit(solution)/shard_map/all_to_all | solution.py:23
  180.3 33.1 %copy-start.4 = (f32[1,2,663]{2,1,0:T(2,128)}, f32[1,2,663]{2,1,0:T(2,128)S(1)}, u32[]{:S(2)}) copy-start(f32[1,2,663]{2,1,0:T(2,128)S(1)} %reduce_max.22) | copy-start | bytes 15916
